TPU v7x, 32 devices: a whole 2x2x4 slice. The times are simulated.
32 devices in a mesh: cuts: 4 (over x, core), exp: 2 (over y), fsdp: 4 (over z).
Axes of the slice: x: 2, y: 2, z: 4, core: 2. Of those that a mesh axis runs over, the one named last changes fastest.
Arguments:
- tokens: bfloat16 [4096, 4096], P(('cuts', 'exp', 'fsdp')), may hold values from -6 to 6
- out_grad: bfloat16 [4096, 4096], P(('cuts', 'exp', 'fsdp')), may hold values from -6 to 6
- expert_ids: int32 [4096, 2], P(('cuts', 'exp', 'fsdp')), may hold values from 0 to 7, as said below
- gate_probs: bfloat16 [4096, 2], P(('cuts', 'exp', 'fsdp')), may hold values from 0.049804688 to 0.94921875
- params: float32 [3, 8, 4096, 256], P(None, 'exp', ('cuts', 'fsdp')), may hold values from -0.1875 to 0.1875
- moment_first: float32 [3, 8, 4096, 256], P(None, 'exp', ('cuts', 'fsdp')), may hold values from -60 to 60
- moment_second: float32 [3, 8, 4096, 256], P(None, 'exp', ('cuts', 'fsdp')), may hold values from 64 to 1024
Outputs:
- token_grad: bfloat16 [4096, 4096], P(('cuts', 'exp', 'fsdp'))
- gate_grad: bfloat16 [4096, 2], P(('cuts', 'exp', 'fsdp'))
- new_params: float32 [3, 8, 4096, 256], P(None, 'exp', ('cuts', 'fsdp'))
- new_first: float32 [3, 8, 4096, 256], P(None, 'exp', ('cuts', 'fsdp'))
- new_second: float32 [3, 8, 4096, 256], P(None, 'exp', ('cuts', 'fsdp'))
Inputs may be any that keep to these rules, and one draw needn't show every extreme that they name: `expert_ids`: the two ids of a token differ. Among the tokens of one device no expert is named more than 40 times. Each device names some expert exactly 40 times, and the devices that share their cuts and fsdp indices have one such expert in common.
All inputs are finite; a program needn't handle non-finite values.
Results may differ from a plain program's by a relative error of at most 0.0079.
Values may be sent and summed in bfloat16 or wider, within the bound.
A program may use at most 192 MiB of HBM per device.

v0:
```python
import jax
import jax.numpy as jnp
from jax import lax
from jax.sharding import PartitionSpec as P

EXPERTS = 8


decay_first = 0.9
decay_second = 0.95
correct_first = 1.0 - 0.9**10
correct_second = 1.0 - 0.95**10
epsilon = 1e-08
learn_rate = 0.0003
weight_decay = 0.1


def adam_update(params, gradient, moment_first, moment_second):
    new_first = decay_first * moment_first + (1.0 - decay_first) * gradient
    new_second = decay_second * moment_second + (1.0 - decay_second) * gradient * gradient
    stepped = new_first / correct_first / (jnp.sqrt(new_second / correct_second) + epsilon)
    new_params = params - learn_rate * (stepped + weight_decay * params)
    return (new_params, new_first, new_second)


def per_device(tokens, out_grad, expert_ids, gate_probs, params, moment_first, moment_second):
    token_count = tokens.shape[0]
    width = tokens.shape[1]
    local_count = params.shape[1]
    exp_count = lax.axis_size("exp")
    capacity = 10 * token_count // 32
    weights = lax.all_gather(params.astype(jnp.bfloat16), ("cuts", "fsdp"), axis=2, tiled=True)
    flat_ids = expert_ids.reshape(-1)
    onehot = (flat_ids[:, None] == jnp.arange(EXPERTS, dtype=jnp.int32)[None, :]).astype(jnp.int32)
    before = jnp.cumsum(onehot, axis=0) - onehot
    position = jnp.sum(before * onehot, axis=1)
    holder = flat_ids // local_count
    local_index = flat_ids % local_count
    target = (local_index * exp_count + holder) * capacity + position
    placement = (
        target[:, None] == jnp.arange(EXPERTS * capacity, dtype=jnp.int32)[None, :]
    ).astype(jnp.bfloat16)
    token_place = jnp.sum(placement.reshape(token_count, 2, EXPERTS * capacity), axis=1)
    send_inputs = jnp.einsum(
        "tc,td->cd", token_place, tokens, preferred_element_type=jnp.float32
    ).astype(jnp.bfloat16)
    send_upstream = jnp.einsum(
        "tc,td->cd", token_place, out_grad, preferred_element_type=jnp.float32
    ).astype(jnp.bfloat16)
    send_gates = jnp.einsum(
        "pc,p->c", placement, gate_probs.reshape(-1), preferred_element_type=jnp.float32
    ).astype(jnp.bfloat16)
    layout = (local_count, exp_count, capacity)
    arrived_inputs, arrived_upstream, arrived_gates = (
        lax.all_to_all(
            send_inputs.reshape(layout + (width,)), "exp", split_axis=1, concat_axis=1, tiled=True
        ),
        lax.all_to_all(
            send_upstream.reshape(layout + (width,)), "exp", split_axis=1, concat_axis=1, tiled=True
        ),
        lax.all_to_all(
            send_gates.reshape(layout + (1,)), "exp", split_axis=1, concat_axis=1, tiled=True
        ),
    )
    slot_count = exp_count * capacity
    arrived_inputs = arrived_inputs.reshape(local_count, slot_count, width)
    arrived_upstream = arrived_upstream.reshape(local_count, slot_count, width)
    gate_values = arrived_gates.reshape(local_count, slot_count, 1).astype(jnp.float32)
    w_gate = weights[0]
    w_up = weights[1]
    w_down = weights[2]
    pre_gate = jnp.einsum(
        "esd,edf->esf", arrived_inputs, w_gate, preferred_element_type=jnp.float32
    )
    pre_up = jnp.einsum("esd,edf->esf", arrived_inputs, w_up, preferred_element_type=jnp.float32)
    sigmoid_gate = jax.nn.sigmoid(pre_gate)
    activated = pre_gate * sigmoid_gate
    hidden = activated * pre_up
    projected = jnp.einsum(
        "esd,edf->esf", arrived_upstream, w_down, preferred_element_type=jnp.float32
    )
    slot_gate = jnp.sum(hidden * projected, axis=2, keepdims=True).astype(jnp.bfloat16)
    delta_hidden = gate_values * projected
    delta_gate = (
        delta_hidden * pre_up * sigmoid_gate * (1.0 + pre_gate * (1.0 - sigmoid_gate))
    ).astype(jnp.bfloat16)
    delta_up = (delta_hidden * activated).astype(jnp.bfloat16)
    scaled = (gate_values * arrived_upstream.astype(jnp.float32)).astype(jnp.bfloat16)
    slot_grads = (
        jnp.einsum("esf,edf->esd", delta_gate, w_gate, preferred_element_type=jnp.float32)
        + jnp.einsum("esf,edf->esd", delta_up, w_up, preferred_element_type=jnp.float32)
    ).astype(jnp.bfloat16)
    returned_grads, returned_gate = (
        lax.all_to_all(
            slot_grads.reshape(layout + (width,)), "exp", split_axis=1, concat_axis=1, tiled=True
        ),
        lax.all_to_all(
            slot_gate.reshape(layout + (1,)), "exp", split_axis=1, concat_axis=1, tiled=True
        ),
    )
    grad_gate = jnp.einsum(
        "esd,esf->edf", arrived_inputs, delta_gate, preferred_element_type=jnp.float32
    )
    grad_up = jnp.einsum(
        "esd,esf->edf", arrived_inputs, delta_up, preferred_element_type=jnp.float32
    )
    grad_down = jnp.einsum(
        "esd,esf->edf", scaled, hidden.astype(jnp.bfloat16), preferred_element_type=jnp.float32
    )
    returned_grads = returned_grads.reshape(EXPERTS * capacity, width)
    returned_gate = returned_gate.reshape(EXPERTS * capacity, 1)
    token_grad = jnp.einsum(
        "tc,cd->td", token_place, returned_grads, preferred_element_type=jnp.float32
    ).astype(jnp.bfloat16)
    gate_grad = jnp.einsum(
        "pc,cx->px", placement, returned_gate, preferred_element_type=jnp.float32
    )
    gate_grad = gate_grad.reshape(token_count, 2).astype(jnp.bfloat16)
    reduced = (
        lax.psum_scatter(grad_gate, ("cuts", "fsdp"), scatter_dimension=1, tiled=True),
        lax.psum_scatter(grad_up, ("cuts", "fsdp"), scatter_dimension=1, tiled=True),
        lax.psum_scatter(grad_down, ("cuts", "fsdp"), scatter_dimension=1, tiled=True),
    )
    gradient = jnp.stack([reduced[0], reduced[1], reduced[2]])
    new_params, new_first, new_second = adam_update(params, gradient, moment_first, moment_second)
    return (token_grad, gate_grad, new_params, new_first, new_second)


def solution(mesh):
    return jax.shard_map(
        per_device,
        mesh=mesh,
        in_specs=(
            P(("cuts", "exp", "fsdp"), None),
            P(("cuts", "exp", "fsdp"), None),
            P(("cuts", "exp", "fsdp"), None),
            P(("cuts", "exp", "fsdp"), None),
            P(None, "exp", ("cuts", "fsdp"), None),
            P(None, "exp", ("cuts", "fsdp"), None),
            P(None, "exp", ("cuts", "fsdp"), None),
        ),
        out_specs=(
            P(("cuts", "exp", "fsdp"), None),
            P(("cuts", "exp", "fsdp"), None),
            P(None, "exp", ("cuts", "fsdp"), None),
            P(None, "exp", ("cuts", "fsdp"), None),
            P(None, "exp", ("cuts", "fsdp"), None),
        ),
        check_vma=False,
    )
```

profile of v0, /device:TPU:0, one launch (start us, length us, event | category | flops | bytes accessed | tf_op | source)
XLA Modules:
  0.0 720.5 jit_solution(18314282270735941708)
XLA Ops:
  7.2 0.0 copy-start
  7.2 0.0 all-gather.2.cloned.1.call-start
  7.2 3.3 convert_element_type.82
  10.5 0.0 all-gather.2.cloned.1.call-update
  10.6 0.1 copy.63
  10.7 0.1 eq.69
  10.8 0.1 eq.73
  11.0 0.1 copy.72
  11.1 0.1 reshape.182
  11.3 0.6 reduce-window.6
  11.9 0.2 slice_reduce_fusion
  12.1 0.1 fusion.30
  12.2 0.3 convolution_reduce_fusion
  12.5 0.1 reshape.173
  12.6 0.6 copy.73
  13.2 4.3 all-to-all-start
  17.4 0.1 reduce_sum.33
  17.6 0.1 copy.66
  17.7 0.1 fusion.24
  17.8 0.1 copy.71
  17.9 0.1 fusion.17
  18.0 0.8 convolution_convert_fusion
  18.8 1.8 copy.77
  20.6 0.6 all-to-all-done
  21.2 3.9 all-to-all-start.2
  25.1 2.1 convolution_convert_fusion.1
  27.2 1.8 copy.75
  29.0 26.4 %all-to-all-done.2 = bf16[4,2,40,4096]{3,2,0,1:T(8,128)(2,1)S(1)} async-done(((bf16[4,2,40,4096]{3,2,0,1:T(8,128)(2,1)}), bf16[4,2,40,4096]{3,2,0,1:T(8,128)(2,1)S(1)}, u32[]{:S(2)}, u32[]{:S(2)}) %all-to-all-start.2) | async-done | bytes 2621472 | tf_op jit(solution)/shard_map/all_to_all | solution.py:55
  55.4 5.1 all-to-all-start.1
  60.5 0.0 reduce-scatter.8.cloned.1.call-start
  60.6 0.1 reshape.181
  60.6 1.9 copy.78
  62.6 27.5 %all-to-all-done.1 = bf16[4,2,40,4096]{3,2,0,1:T(8,128)(2,1)} async-done(((bf16[4,2,40,4096]{3,2,0,1:T(8,128)(2,1)}), bf16[4,2,40,4096]{3,2,0,1:T(8,128)(2,1)}, u32[]{:S(2)}, u32[]{:S(2)}) %all-to-all-start.1) | async-done | bytes 2621472 | tf_op jit(solution)/shard_map/all_to_all | solution.py:58
  90.1 3.6 copy.76
  93.7 55.5 %all-gather.2.cloned.1.call-done = bf16[3,4,4096,256]{3,2,1,0:T(8,128)(2,1)} async-done(((bf16[3,4,256,256]{3,2,1,0:T(8,128)(2,1)}), bf16[3,4,4096,256]{3,2,1,0:T(8,128)(2,1)}) %all-gather.2.cloned.1.call-update) | async-done | bytes 25165840 | tf_op jit(solution)/shard_map/all_gather | solution.py:32
  149.2 4.9 fusion.4
  154.1 0.0 copy-start.2
  154.1 5.1 fusion.2
  159.2 8.2 %fusion.8 = f32[4,4096,256]{2,1,0:T(8,128)} fusion(bf16[4,80,4096]{2,1,0:T(8,128)(2,1)S(1)} %bitcast.70, f32[4,80]{1,0:T(4,128)S(1)} %reshape.181, f32[4,80,256]{2,1,0:T(8,128)S(1)} %fusion.2, f32[4,80,256]{2,1,0:T(8,128)S(1)} %fusion.4), kind=kOutput, calls=%fused_computation.19 | convolution fusion | flops 675512320 | bytes 20055296 | tf_op jit(solution)/shard_map/esd,esf->edf/dot_general | solution.py:107
  167.4 0.0 reduce-scatter.8.cloned.1.call-update
  167.4 0.2 reduce-scatter.4.cloned.1.call-start
  167.7 5.8 multiply_reduce_fusion
  173.5 11.5 %fusion.36 = f32[4,4096,256]{2,1,0:T(8,128)} fusion(bf16[4,80,4096]{2,1,0:T(8,128)(2,1)S(1)} %bitcast.65, bf16[4,80,256]{2,1,0:T(8,128)(2,1)S(1)} %get-tuple-element.9), kind=kOutput, calls=%fused_computation.69 | convolution fusion | flops 671088640 | bytes 19562496 | tf_op jit(solution)/shard_map/esd,esf->edf/dot_general | solution.py:101
  185.0 0.0 reduce-scatter.4.cloned.1.call-update
  185.0 0.0 reduce-scatter.6.cloned.1.call-start
  185.1 10.6 %fusion.37 = f32[4,4096,256]{2,1,0:T(8,128)} fusion(bf16[4,80,4096]{2,1,0:T(8,128)(2,1)S(1)} %bitcast.66, bf16[4,80,256]{2,1,0:T(8,128)(2,1)S(1)} %get-tuple-element.10), kind=kOutput, calls=%fused_computation.70 | convolution fusion | flops 671088640 | bytes 19562496 | tf_op jit(solution)/shard_map/esd,esf->edf/dot_general | solution.py:104
  195.7 0.0 reduce-scatter.6.cloned.1.call-update
  195.7 0.1 convert_element_type.89
  195.8 0.6 copy.82
  196.3 3.2 all-to-all-start.4
  199.6 6.0 fusion.1
  205.6 6.1 fusion.6
  211.7 1.7 copy.79
  213.3 3.9 all-to-all-start.3
  217.2 0.1 reshape.184
  217.3 0.1 fusion.15
  217.4 0.5 convert_element_type.90
  218.0 30.4 %all-to-all-done.3 = bf16[4,2,40,4096]{3,2,0,1:T(8,128)(2,1)S(1)} async-done(((bf16[4,2,40,4096]{3,2,0,1:T(8,128)(2,1)}), bf16[4,2,40,4096]{3,2,0,1:T(8,128)(2,1)S(1)}, u32[]{:S(2)}, u32[]{:S(2)}) %all-to-all-start.3) | async-done | bytes 2621472 | tf_op jit(solution)/shard_map/all_to_all | solution.py:94
  248.4 0.2 copy.80
  248.6 1.7 convolution_convert_fusion.2
  250.3 94.5 %reduce-scatter.8.cloned.1.call-done = f32[4,256,256]{2,1,0:T(8,128)} async-done(((f32[4,4096,256]{2,1,0:T(8,128)}), f32[4,256,256]{2,1,0:T(8,128)}) %reduce-scatter.8.cloned.1.call-update) | async-done | bytes 1048592 | tf_op jit(solution)/shard_map/reduce_scatter | solution.py:122
  344.8 180.6 %reduce-scatter.4.cloned.1.call-done = f32[4,256,256]{2,1,0:T(8,128)} async-done(((f32[4,4096,256]{2,1,0:T(8,128)}), f32[4,256,256]{2,1,0:T(8,128)}) %reduce-scatter.4.cloned.1.call-update) | async-done | bytes 1048592 | tf_op jit(solution)/shard_map/reduce_scatter | solution.py:120
  525.4 180.5 %reduce-scatter.6.cloned.1.call-done = f32[4,256,256]{2,1,0:T(8,128)} async-done(((f32[4,4096,256]{2,1,0:T(8,128)}), f32[4,256,256]{2,1,0:T(8,128)}) %reduce-scatter.6.cloned.1.call-update) | async-done | bytes 1048592 | tf_op jit(solution)/shard_map/reduce_scatter | solution.py:121
  705.9 8.0 %multiply_subtract_fusion = (f32[3,4,256,256]{3,2,1,0:T(8,128)}, f32[3,4,256,256]{3,2,1,0:T(8,128)}, f32[3,4,256,256]{3,2,1,0:T(8,128)}) fusion(f32[3,4,256,256]{3,2,1,0:T(8,128)} %param.11, f32[1,4,256,256]{3,2,1,0:T(8,128)} %bitcast.73, f32[1,4,256,256]{3,2,1,0:T(8,128)} %bitcast.75, f32[1,4,256,256]{3,2,1,0:T(8,128)} %bitcast.74, ...), kind=kLoop, calls=%fused_computation.17 | loop fusion | flops 13369344 | bytes 22020096 | tf_op jit(solution)/shard_map/sub | solution.py:22
  (20 shorter events, 0.1 us)
Async XLA Ops:
  7.2 10.8 %copy-start = (bf16[128,4096]{1,0:T(8,128)(2,1)S(1)}, bf16[128,4096]{1,0:T(8,128)(2,1)}, u32[]{:S(2)}) copy-start(bf16[128,4096]{1,0:T(8,128)(2,1)} %param.7) | copy-start | bytes 3145732
  7.2 3.4 copy-start.5
  7.2 3.8 copy-start.6
  7.2 142.0 %all-gather.2.cloned.1.call-start = ((), (), s32[]{:S(2)}) async-start(), calls=%async_computation.8 | async-start | bytes 26738688 | tf_op jit(solution)/shard_map/all_gather | solution.py:32
  13.2 8.0 %all-to-all-start = ((bf16[4,2,40,1]{2,0,3,1:T(4,128)(2,1)}), bf16[4,2,40,1]{2,0,3,1:T(4,128)(2,1)S(1)}, u32[]{:S(2)}, u32[]{:S(2)}) async-start(bf16[4,2,40,1]{2,0,3,1:T(4,128)(2,1)} %copy.73), calls=%async_computation | async-start | bytes 4096 | tf_op jit(solution)/shard_map/all_to_all | solution.py:61
  21.2 34.2 %all-to-all-start.2 = ((bf16[4,2,40,4096]{3,2,0,1:T(8,128)(2,1)}), bf16[4,2,40,4096]{3,2,0,1:T(8,128)(2,1)S(1)}, u32[]{:S(2)}, u32[]{:S(2)}) async-start(bf16[4,2,40,4096]{3,2,0,1:T(8,128)(2,1)} %copy.77), calls=%async_computation.2 | async-start | bytes 5242880 | tf_op jit(solution)/shard_map/all_to_all | solution.py:55
  55.4 5.2 copy-start.3
  55.4 34.7 %all-to-all-start.1 = ((bf16[4,2,40,4096]{3,2,0,1:T(8,128)(2,1)}), bf16[4,2,40,4096]{3,2,0,1:T(8,128)(2,1)}, u32[]{:S(2)}, u32[]{:S(2)}) async-start(bf16[4,2,40,4096]{3,2,0,1:T(8,128)(2,1)} %copy.75), calls=%async_computation.1 | async-start | bytes 5242880 | tf_op jit(solution)/shard_map/all_to_all | solution.py:58
  60.5 284.4 %reduce-scatter.8.cloned.1.call-start = ((), (), s32[]{:S(2)}) async-start(), calls=%async_computation.11 | async-start | bytes 17825792 | tf_op jit(solution)/shard_map/reduce_scatter | solution.py:122
  154.1 5.1 copy-start.2
  159.2 8.2 %copy-start.4 = (f32[4,80,256]{2,1,0:T(8,128)}, f32[4,80,256]{2,1,0:T(8,128)S(1)}, u32[]{:S(2)}) copy-start(f32[4,80,256]{2,1,0:T(8,128)S(1)} %fusion.2) | copy-start | bytes 983044
  167.4 358.0 %reduce-scatter.4.cloned.1.call-start = ((), (), s32[]{:S(2)}) async-start(), calls=%async_computation.9 | async-start | bytes 17825792 | tf_op jit(solution)/shard_map/reduce_scatter | solution.py:120
  185.0 520.9 %reduce-scatter.6.cloned.1.call-start = ((), (), s32[]{:S(2)}) async-start(), calls=%async_computation.10 | async-start | bytes 17825792 | tf_op jit(solution)/shard_map/reduce_scatter | solution.py:121
  196.3 17.0 %all-to-all-start.4 = ((bf16[4,2,40,1]{2,0,3,1:T(4,128)(2,1)}), bf16[4,2,40,1]{2,0,3,1:T(4,128)(2,1)S(1)}, u32[]{:S(2)}, u32[]{:S(2)}) async-start(bf16[4,2,40,1]{2,0,3,1:T(4,128)(2,1)} %copy.82), calls=%async_computation.4 | async-start | bytes 4096 | tf_op jit(solution)/shard_map/all_to_all | solution.py:97
  213.3 35.1 %all-to-all-start.3 = ((bf16[4,2,40,4096]{3,2,0,1:T(8,128)(2,1)}), bf16[4,2,40,4096]{3,2,0,1:T(8,128)(2,1)S(1)}, u32[]{:S(2)}, u32[]{:S(2)}) async-start(bf16[4,2,40,4096]{3,2,0,1:T(8,128)(2,1)} %copy.79), calls=%async_computation.3 | async-start | bytes 5242880 | tf_op jit(solution)/shard_map/all_to_all | solution.py:94
  705.9 8.0 %copy-start.1 = (bf16[128,4096]{1,0:T(8,128)(2,1)S(1)}, bf16[128,4096]{1,0:T(8,128)(2,1)}, u32[]{:S(2)}) copy-start(bf16[128,4096]{1,0:T(8,128)(2,1)} %param.7) | copy-start | bytes 3145732
Sparse Core Ops, SparseCore 0:
  10.7 138.4 all-gather.1
  167.5 177.2 reduce-scatter.7
  349.0 176.4 reduce-scatter.3
  529.4 176.4 reduce-scatter.5
where the time goes:
time: 721 us; the launch traced here: 720 us
  waiting for transfers between devices  596 us (83%)
  matrix products  63.2 us (9%)
  starting transfers between devices  20.6 us (3%)
  between operations  14 us (2%)
  local copies, waits for them, and re-layouts  13.7 us (2%)
  other arithmetic  12.7 us (2%)
    reduce_scatter x1, waiting for transfers between devices, per_device(): lax.psum_scatter(grad_gate, ('cuts', 'fsdp'), scatter_dimension=1, tiled=...  181 us
    reduce_scatter x1, waiting for transfers between devices, per_device(): lax.psum_scatter(grad_up, ('cuts', 'fsdp'), scatter_dimension=1, tiled=True)  180 us
    reduce_scatter x1, waiting for transfers between devices, per_device(): lax.psum_scatter(grad_down, ('cuts', 'fsdp'), scatter_dimension=1, tiled=...  94.5 us
    all_gather x1, waiting for transfers between devices, per_device(): lax.all_gather(params.astype(jnp.bfloat16), ('cuts', 'fsdp'), axis=2, til...  55.5 us
    all_to_all x1, waiting for transfers between devices, per_device(): lax.all_to_all(slot_grads.reshape(layout + (width,)), 'exp', split_axis=1...  30.4 us
    all_to_all x1, waiting for transfers between devices, per_device(): lax.all_to_all(send_upstream.reshape(layout + (width,)), 'exp', split_axi...  27.5 us
    all_to_all x1, waiting for transfers between devices, per_device(): lax.all_to_all(send_inputs.reshape(layout + (width,)), 'exp', split_axis=...  26.4 us
  transfers between devices with their start and end apart: 9, of which 8 were waited for; matrix products, arithmetic and copies ran while one was open for 8% of the time, Pallas kernels for 0%

commit v1 on v0

v1 whole, which is shorter than its diff:
```python
import jax
import jax.numpy as jnp
from jax import lax
from jax.sharding import PartitionSpec as P

EXPERTS = 8


decay_first = 0.9
decay_second = 0.95
correct_first = 1.0 - 0.9**10
correct_second = 1.0 - 0.95**10
epsilon = 1e-08
learn_rate = 0.0003
weight_decay = 0.1
GROUP = ("cuts", "fsdp")


def adam_update(params, gradient, moment_first, moment_second):
    new_first = decay_first * moment_first + (1.0 - decay_first) * gradient
    new_second = decay_second * moment_second + (1.0 - decay_second) * gradient * gradient
    stepped = new_first / correct_first / (jnp.sqrt(new_second / correct_second) + epsilon)
    new_params = params - learn_rate * (stepped + weight_decay * params)
    return (new_params, new_first, new_second)


def per_device(tokens, out_grad, expert_ids, gate_probs, params, moment_first, moment_second):
    token_count, width = tokens.shape
    local = params.shape[1]
    rows = params.shape[2]
    hidden_units = params.shape[3]
    shares = width // rows
    exp_count = lax.axis_size("exp")
    capacity = 10 * token_count // 32
    me = lax.axis_index("exp")
    local_slots = local * capacity

    weights = params.astype(jnp.bfloat16)
    w_in = jnp.concatenate([weights[0], weights[1]], axis=2)
    w_down = weights[2]

    cores = 2
    cuts = lax.axis_size("cuts")
    shards = lax.axis_size("fsdp")
    chips = cuts // cores
    core_groups = [[chip * cores + core for core in range(cores)] for chip in range(chips)]
    chip_groups = [
        [(chip * cores + core) * shards + shard for chip in range(chips) for shard in range(shards)]
        for core in range(cores)
    ]

    def spread(array):
        parts = array.reshape(array.shape[0], shares, rows).transpose(1, 0, 2)
        return parts

    def exchange(parts):
        parts = lax.all_to_all(parts, GROUP, split_axis=0, concat_axis=0, tiled=True)
        return lax.all_gather(parts, "exp", axis=1, tiled=False)

    flat_ids = expert_ids.reshape(-1)
    onehot = (flat_ids[:, None] == jnp.arange(EXPERTS, dtype=jnp.int32)).astype(jnp.int32)
    before = jnp.cumsum(onehot, axis=0) - onehot
    position = jnp.sum(before * onehot, axis=1)
    extra = jnp.concatenate(
        [flat_ids.astype(jnp.bfloat16), position.astype(jnp.bfloat16), gate_probs.reshape(-1)]
    )
    extra_rows = extra.shape[0] // rows
    padded = -(-extra_rows // 8) * 8
    extra = jnp.pad(extra.reshape(extra_rows, rows), ((0, padded - extra_rows), (0, 0)))
    extra = jnp.broadcast_to(extra[None], (shares, padded, rows))

    sources = shares * exp_count
    token_parts = exchange(jnp.concatenate([spread(tokens), extra], axis=1))
    upstream_parts = exchange(spread(out_grad))
    everyone = token_parts[:, :, token_count : token_count + extra_rows, :]
    everyone = everyone.reshape(sources, 3, token_count, 2)
    ids = everyone[:, 0].astype(jnp.int32)
    all_slots = ids * capacity + everyone[:, 1].astype(jnp.int32) - me * local_slots
    all_gates = everyone[:, 2].astype(jnp.float32)
    columns = jnp.arange(local_slots, dtype=jnp.int32)
    place = (all_slots[:, :, :, None] == columns).astype(jnp.bfloat16).sum(axis=2)

    def pick(array):
        array = array[:, :, :token_count].reshape(sources, token_count, rows)
        picked = jnp.einsum("ntc,ntd->ncd", place, array, preferred_element_type=jnp.bfloat16)
        picked = picked.reshape(sources, local, capacity, rows).transpose(1, 0, 2, 3)
        return picked.reshape(local, sources * capacity, rows)

    inputs = pick(token_parts)
    upstream = pick(upstream_parts)

    def partial_sums(left, right):
        out = jnp.einsum("esd,edf->esf", left, right, preferred_element_type=jnp.float32)
        out = out.astype(jnp.bfloat16)
        out = out.reshape(local, chips, cores, shards, exp_count * capacity, right.shape[2])
        out = out.transpose(2, 1, 3, 0, 4, 5)
        out = lax.all_to_all(
            out, "cuts", split_axis=0, concat_axis=0, tiled=True, axis_index_groups=core_groups
        )
        out = jnp.sum(out.astype(jnp.float32), axis=0).astype(jnp.bfloat16)
        out = out.reshape((chips * shards,) + out.shape[2:])
        out = lax.all_to_all(
            out, GROUP, split_axis=0, concat_axis=0, tiled=True, axis_index_groups=chip_groups
        )
        return jnp.sum(out.astype(jnp.float32), axis=0)

    pre = partial_sums(inputs, w_in)
    projected = partial_sums(upstream, w_down)
    pre_gate = pre[:, :, :hidden_units]
    pre_up = pre[:, :, hidden_units:]

    start = lax.axis_index(GROUP) * exp_count
    my_slots = lax.dynamic_slice_in_dim(all_slots, start, exp_count, axis=0)
    my_gates = lax.dynamic_slice_in_dim(all_gates, start, exp_count, axis=0)
    my_place = (my_slots[:, :, :, None] == columns).astype(jnp.float32)
    gates = jnp.sum(my_place * my_gates[:, :, :, None], axis=(1, 2))
    gates = gates.reshape(exp_count, local, capacity).transpose(1, 0, 2)
    gates = gates.reshape(local, exp_count * capacity, 1)

    sigmoid_gate = jax.nn.sigmoid(pre_gate)
    activated = pre_gate * sigmoid_gate
    hidden = activated * pre_up
    slot_gate = jnp.sum(hidden * projected, axis=2)
    delta_hidden = gates * projected
    delta_gate = delta_hidden * pre_up * sigmoid_gate * (1.0 + pre_gate * (1.0 - sigmoid_gate))
    delta_up = delta_hidden * activated
    deltas = jnp.concatenate([delta_gate, delta_up, gates * hidden], axis=2).astype(jnp.bfloat16)
    deltas = lax.all_gather(deltas, GROUP, axis=0, tiled=False)
    deltas = deltas.transpose(1, 0, 2, 3).reshape(local, sources * capacity, 3 * hidden_units)
    delta_in = deltas[:, :, : 2 * hidden_units]
    scaled_hidden = deltas[:, :, 2 * hidden_units :]

    slot_gate = slot_gate.reshape(local, exp_count, capacity).transpose(1, 0, 2)
    slot_gate = slot_gate.reshape(exp_count, 1, 1, local_slots)
    gate_part = jnp.sum(my_place * slot_gate, axis=3)
    gate_part = gate_part.astype(jnp.bfloat16).reshape(exp_count, token_count * 2)
    gate_part = lax.all_to_all(gate_part, "exp", split_axis=0, concat_axis=0, tiled=True)
    gate_grad = jnp.sum(gate_part.astype(jnp.float32), axis=0).astype(jnp.bfloat16)
    gate_grad = gate_grad.reshape(token_count, 2)

    slot_grads = jnp.einsum("esf,edf->esd", delta_in, w_in, preferred_element_type=jnp.float32)
    slot_grads = slot_grads.astype(jnp.bfloat16).reshape(local, sources, capacity, rows)
    slot_grads = slot_grads.transpose(1, 0, 2, 3).reshape(sources, local_slots, rows)
    returned = jnp.einsum("ntc,ncd->ntd", place, slot_grads, preferred_element_type=jnp.bfloat16)
    returned = returned.reshape(shares, exp_count, token_count, rows)
    returned = lax.all_to_all(returned, "exp", split_axis=1, concat_axis=1, tiled=True)
    returned = jnp.sum(returned.astype(jnp.float32), axis=1).astype(jnp.bfloat16)
    returned = lax.all_to_all(returned, GROUP, split_axis=0, concat_axis=0, tiled=True)
    token_grad = returned.transpose(1, 0, 2).reshape(token_count, width)

    grad_in = jnp.einsum("esd,esf->edf", inputs, delta_in, preferred_element_type=jnp.float32)
    grad_down = jnp.einsum(
        "esd,esf->edf", upstream, scaled_hidden, preferred_element_type=jnp.float32
    )
    gradient = jnp.stack([grad_in[:, :, :hidden_units], grad_in[:, :, hidden_units:], grad_down])
    new_params, new_first, new_second = adam_update(params, gradient, moment_first, moment_second)
    return (token_grad, gate_grad, new_params, new_first, new_second)


def solution(mesh):
    tokens_spec = P(("cuts", "exp", "fsdp"), None)
    weights_spec = P(None, "exp", ("cuts", "fsdp"), None)
    return jax.shard_map(
        per_device,
        mesh=mesh,
        in_specs=(tokens_spec,) * 4 + (weights_spec,) * 3,
        out_specs=(tokens_spec,) * 2 + (weights_spec,) * 3,
        check_vma=False,
    )
```

time: 721 us -> 407 us (0.56)
  waiting for transfers between devices: 596 us -> 192 us
  blocking collectives: 0 us -> 81.7 us
  matrix products: 63.2 us -> 22.6 us
  local copies, waits for them, and re-layouts: 13.7 us -> 43.4 us
  other arithmetic: 12.7 us -> 29.3 us
    reduce_scatter x3 -> x0, waiting for transfers between devices: 456 us -> none  [the longest x1 181 us: per_device(): lax.psum_scatter(grad_gate, ('cuts', 'fsdp'), scatter_dimension=1, tiled=...]
    all_to_all x0 -> x4, blocking collectives: none -> 81.7 us  [the longest x2 65.9 us: exchange(): lax.all_to_all(parts, GROUP, split_axis=0, concat_axis=0, tiled=True)]
    dot_general x13 -> x8, matrix products: 63.2 us -> 22.6 us  [the longest x2 5.71 us: pick(): jnp.einsum('ntc,ntd->ncd', place, array, preferred_element_type=jnp.bfloa...]
    all_to_all x5, waiting for transfers between devices: 85.1 us -> 118 us  [the longest x2 80.6 us: partial_sums(): lax.all_to_all(out, GROUP, split_axis=0, concat_axis=0, tiled=True, axis_...]
    all_gather x1 -> x3, waiting for transfers between devices: 55.5 us -> 74.5 us  [the longest x1 62.3 us: per_device(): deltas = lax.all_gather(deltas, GROUP, axis=0, tiled=False)]
    reduce_sum x1 -> x9, other arithmetic: 0.06 us -> 17.7 us  [the longest x2 9.5 us: partial_sums(): out = jnp.sum(out.astype(jnp.float32), axis=0).astype(jnp.bfloat16)]
    reshape x5 -> x14, local copies, waits for them, and re-layouts: 5.92 us -> 18.9 us  [the longest x1 6.79 us: per_device(): everyone = everyone.reshape(sources, 3, token_count, 2)]
    unnamed x16 -> x32, local copies, waits for them, and re-layouts: 0.29 us -> 9.12 us
  transfers between devices with their start and end apart: 9 -> 8, of which waited for: 8 -> 6; matrix products, arithmetic and copies ran while one was open for 8% -> 14% of each run, Pallas kernels for 0% -> 0%
where the time goes in v1:
time: 407 us; the launch traced here: 406 us
  waiting for transfers between devices  192 us (47%)
  blocking collectives  81.7 us (20%)
  local copies, waits for them, and re-layouts  43.4 us (11%)
  other arithmetic  29.3 us (7%)
  starting transfers between devices  22.6 us (6%)
  matrix products  22.6 us (6%)
  between operations  14.2 us (3%)
    all_to_all x2, waiting for transfers between devices, partial_sums(): lax.all_to_all(out, GROUP, split_axis=0, concat_axis=0, tiled=True, axis_...  80.6 us
    all_to_all x2, blocking collectives, exchange(): lax.all_to_all(parts, GROUP, split_axis=0, concat_axis=0, tiled=True)  65.9 us
    all_gather x1, waiting for transfers between devices, per_device(): deltas = lax.all_gather(deltas, GROUP, axis=0, tiled=False)  62.3 us
    all_to_all x1, waiting for transfers between devices, per_device(): lax.all_to_all(returned, 'exp', split_axis=1, concat_axis=1, tiled=True)  24.8 us
    all_to_all x2, blocking collectives, partial_sums(): lax.all_to_all(out, 'cuts', split_axis=0, concat_axis=0, tiled=True, axis...  15.8 us
    all_gather x2, waiting for transfers between devices, exchange(): return lax.all_gather(parts, 'exp', axis=1, tiled=False)  12.2 us
    all_to_all x1, waiting for transfers between devices, per_device(): lax.all_to_all(returned, GROUP, split_axis=0, concat_axis=0, tiled=True)  12.2 us
    all_to_all x2, starting transfers between devices, partial_sums(): lax.all_to_all(out, GROUP, split_axis=0, concat_axis=0, tiled=True, axis_...  9.89 us
  transfers between devices with their start and end apart: 8, of which 6 were waited for; matrix products, arithmetic and copies ran while one was open for 14% of the time, Pallas kernels for 0%

profile of v1, /device:TPU:0, one launch (start us, length us, event | category | flops | bytes accessed | tf_op | source)
XLA Modules:
  0.0 406.0 jit_solution(9690866819716515778)
XLA Ops:
  7.2 0.8 copy.205
  8.3 0.8 copy.207
  9.2 0.6 reduce-window.6
  10.4 1.6 copy.204
  12.2 0.4 pad_maximum_fusion.1
  12.7 1.5 copy.209
  14.2 35.7 %all_to_all.46 = bf16[16,136,256]{2,1,0:T(8,128)(2,1)S(1)} all-to-all(bf16[16,136,256]{2,1,0:T(8,128)(2,1)S(1)} %copy.209), channel_id=1, replica_groups=mesh['cuts'=4,'exp'=2,'fsdp'=4] {'cuts','fsdp'}, dimensions={0} | all-to-all | bytes 2228224 | tf_op jit(solution)/shard_map/all_to_all | solution.py:57
  49.9 1.2 copy.210
  51.2 1.5 copy.251
  52.7 30.2 %all_to_all.47 = bf16[16,128,256]{2,1,0:T(8,128)(2,1)} all-to-all(bf16[16,128,256]{2,1,0:T(8,128)(2,1)S(1)} %bitcast.109), channel_id=1, replica_groups=mesh['cuts'=4,'exp'=2,'fsdp'=4] {'cuts','fsdp'}, dimensions={0} | all-to-all | bytes 2097152 | tf_op jit(solution)/shard_map/all_to_all | solution.py:57
  82.9 1.3 convert_element_type.97
  84.2 2.2 slice_bitcast_fusion.3
  86.5 2.4 copy.211
  88.9 1.6 slice.70
  90.5 6.8 %reshape.194 = bf16[32,3,128,2]{3,2,0,1:T(8,128)(2,1)S(1)} reshape(bf16[16,2,3,256]{3,1,0,2:T(2,128)(2,1)S(1)} %copy.212) | data formatting | bytes 98304 | tf_op jit(solution)/shard_map/reshape | solution.py:76
  97.3 1.9 fusion.38
  99.3 2.2 copy.213
  101.5 0.8 fusion.9
  102.2 2.9 fusion.26
  105.1 1.7 copy.222
  106.8 12.2 %all-gather.10.cloned.1.call-done = bf16[16,256,256]{2,1,0:T(8,128)(2,1)} async-done(((bf16[16,128,256]{2,1,0:T(8,128)(2,1)}), bf16[16,256,256]{2,1,0:T(8,128)(2,1)}) %all-gather.10.cloned.1.call-update) | async-done | bytes 2097168 | tf_op jit(solution)/shard_map/all_gather | solution.py:58
  119.0 2.8 fusion.25
  122.1 2.3 convolution_convert_fusion.1
  124.3 0.2 copy.250
  124.6 6.8 %all_to_all.48 = bf16[2,2,4,4,80,256]{5,4,2,1,3,0:T(8,128)(2,1)} all-to-all(bf16[2,2,4,4,80,256]{5,4,2,1,3,0:T(8,128)(2,1)S(1)} %bitcast.99), channel_id=1, replica_groups={{0,8},{16,24},{1,9},{17,25},{2,10},{18,26},{3,11},{19,27},{4,12},{20,28..., dimensions={0} | all-to-all | bytes 5242880 | tf_op jit(solution)/shard_map/all_to_all | solution.py:97
  131.3 3.6 reduce_sum.117
  135.0 2.6 copy.221
  137.6 2.7 convolution_convert_fusion
  140.3 0.5 copy.249
  140.8 9.1 %all_to_all.49 = bf16[2,2,4,4,80,512]{5,4,2,1,3,0:T(8,128)(2,1)} all-to-all(bf16[2,2,4,4,80,512]{5,4,2,1,3,0:T(8,128)(2,1)S(1)} %bitcast.91), channel_id=1, replica_groups={{0,8},{16,24},{1,9},{17,25},{2,10},{18,26},{3,11},{19,27},{4,12},{20,28..., dimensions={0} | all-to-all | bytes 10485760 | tf_op jit(solution)/shard_map/all_to_all | solution.py:97
  149.9 5.5 %all-to-all-start.3 = ((bf16[8,4,80,256]{3,2,1,0:T(8,128)(2,1)}), bf16[8,4,80,256]{3,2,1,0:T(8,128)(2,1)}, u32[]{:S(2)}, u32[]{:S(2)}) async-start(bf16[8,4,80,256]{3,2,1,0:T(8,128)(2,1)} %copy.221), calls=%async_computation.3 | async-start | bytes 2621440 | tf_op jit(solution)/shard_map/all_to_all | solution.py:102
  155.4 5.9 %reduce_sum.119 = bf16[2,4,4,80,512]{4,3,1,0,2:T(8,128)(2,1)} reduce(bf16[2,2,4,4,80,512]{5,4,2,1,3,0:T(8,128)(2,1)} %all_to_all.49, bf16[]{:T(256)} %constant.42.clone.1), dimensions={0}, to_apply=%region_7.8 | reduce | flops 1310720 | bytes 7864322 | tf_op jit(solution)/shard_map/reduce_sum | solution.py:100
  161.3 3.5 copy.225
  164.8 23.4 %all-to-all-done.3 = bf16[8,4,80,256]{3,2,1,0:T(8,128)(2,1)} async-done(((bf16[8,4,80,256]{3,2,1,0:T(8,128)(2,1)}), bf16[8,4,80,256]{3,2,1,0:T(8,128)(2,1)}, u32[]{:S(2)}, u32[]{:S(2)}) %all-to-all-start.3) | async-done | bytes 1310752 | tf_op jit(solution)/shard_map/all_to_all | solution.py:102
  188.2 4.4 %all-to-all-start.5 = ((bf16[8,4,80,512]{3,2,1,0:T(8,128)(2,1)}), bf16[8,4,80,512]{3,2,1,0:T(8,128)(2,1)}, u32[]{:S(2)}, u32[]{:S(2)}) async-start(bf16[8,4,80,512]{3,2,1,0:T(8,128)(2,1)} %copy.225), calls=%async_computation.5 | async-start | bytes 5242880 | tf_op jit(solution)/shard_map/all_to_all | solution.py:102
  192.8 0.6 add_subtract_fusion
  193.6 1.5 convert_reduce_fusion.1
  195.1 57.2 %all-to-all-done.5 = bf16[8,4,80,512]{3,2,1,0:T(8,128)(2,1)} async-done(((bf16[8,4,80,512]{3,2,1,0:T(8,128)(2,1)}), bf16[8,4,80,512]{3,2,1,0:T(8,128)(2,1)}, u32[]{:S(2)}, u32[]{:S(2)}) %all-to-all-start.5) | async-done | bytes 2621472 | tf_op jit(solution)/shard_map/all_to_all | solution.py:102
  252.3 2.2 convert_reduce_fusion
  255.3 0.2 fusion.18
  255.6 0.8 pad_maximum_fusion.5
  256.7 0.5 broadcast.66
  257.2 0.7 reduce.8
  257.9 0.6 reshape.218
  258.5 3.2 all-to-all-start.8
  261.7 62.3 %all-gather.6.cloned.1.call-done = bf16[16,4,80,768]{3,2,0,1:T(8,128)(2,1)} async-done(((bf16[1,4,80,768]{3,2,0,1:T(8,128)(2,1)}), bf16[16,4,80,768]{3,2,0,1:T(8,128)(2,1)}) %all-gather.6.cloned.1.call-update) | async-done | bytes 7864336 | tf_op jit(solution)/shard_map/all_gather | solution.py:128
  323.9 4.0 fusion.5
  328.0 0.3 copy.228
  328.3 1.0 copy-done.1
  329.3 0.8 fusion.27
  330.1 1.5 copy.229
  331.6 4.8 %all-to-all-start.6 = ((bf16[16,2,128,256]{3,2,0,1:T(8,128)(2,1)}), bf16[16,2,128,256]{3,2,0,1:T(8,128)(2,1)}, u32[]{:S(2)}, u32[]{:S(2)}) async-start(bf16[16,2,128,256]{3,2,0,1:T(8,128)(2,1)} %copy.229), calls=%async_computation.6 | async-start | bytes 4194304 | tf_op jit(solution)/shard_map/all_to_all | solution.py:146
  336.6 0.6 copy.238
  337.2 24.8 %all-to-all-done.6 = bf16[16,2,128,256]{3,2,0,1:T(8,128)(2,1)} async-done(((bf16[16,2,128,256]{3,2,0,1:T(8,128)(2,1)}), bf16[16,2,128,256]{3,2,0,1:T(8,128)(2,1)}, u32[]{:S(2)}, u32[]{:S(2)}) %all-to-all-start.6) | async-done | bytes 2097184 | tf_op jit(solution)/shard_map/all_to_all | solution.py:146
  362.0 3.3 reduce_sum.121
  365.3 4.6 %all-to-all-start.7 = ((bf16[16,128,256]{2,1,0:T(8,128)(2,1)}), bf16[16,128,256]{2,1,0:T(8,128)(2,1)}, u32[]{:S(2)}, u32[]{:S(2)}) async-start(bf16[16,128,256]{2,1,0:T(8,128)(2,1)} %reduce_sum.121), calls=%async_computation.7 | async-start | bytes 2097152 | tf_op jit(solution)/shard_map/all_to_all | solution.py:148
  369.9 4.2 %fusion.1 = f32[4,256,512]{2,1,0:T(8,128)S(1)} fusion(bf16[4,1280,256]{2,1,0:T(8,128)(2,1)S(1)} %bitcast.102, bf16[4,1280,768]{2,1,0:T(8,128)(2,1)} %bitcast.119), kind=kOutput, calls=%fused_computation.6 | convolution fusion | flops 1342177280 | bytes 9961472 | tf_op jit(solution)/shard_map/esd,esf->edf/dot_general | solution.py:151
  374.3 1.5 copy-done.5
  375.8 2.9 fusion.12
  378.8 0.7 copy-done.8
  379.5 4.8 %multiply_subtract_fusion = (f32[3,4,256,256]{3,2,1,0:T(8,128)}, f32[3,4,256,256]{3,2,1,0:T(8,128)}, f32[3,4,256,256]{3,2,1,0:T(8,128)}) fusion(f32[3,4,256,256]{3,2,1,0:T(8,128)S(1)} %copy-done.3, f32[1,4,256,256]{3,2,1,0:T(8,128)S(1)} %fusion.12, f32[1,4,256,256]{3,2,1,0:T(8,128)S(1)} %get-tuple-element.56, f32[1,4,256,256]{3,2,1,0:T(8,128)S(1)} %get-tuple-element.55, ...), kind=kLoop, calls=%fused_computation.14 | loop fusion | flops 13369344 | bytes 22020096 | tf_op jit(solution)/shard_map/sub | solution.py:23
  384.3 12.2 %all-to-all-done.7 = bf16[16,128,256]{2,1,0:T(8,128)(2,1)} async-done(((bf16[16,128,256]{2,1,0:T(8,128)(2,1)}), bf16[16,128,256]{2,1,0:T(8,128)(2,1)}, u32[]{:S(2)}, u32[]{:S(2)}) %all-to-all-start.7) | async-done | bytes 1048608 | tf_op jit(solution)/shard_map/all_to_all | solution.py:148
  396.5 1.6 copy.231
  398.1 1.3 copy.237
  (66 shorter events, 3.4 us)
Async XLA Ops:
  7.2 79.3 %all-gather.8.cloned.1.call-start = ((), (), s32[]{:S(2)}) async-start(), calls=%async_computation.10 | async-start | bytes 3342336 | tf_op jit(solution)/shard_map/all_gather | solution.py:58
  51.2 67.9 %all-gather.10.cloned.1.call-start = ((), (), s32[]{:S(2)}) async-start(), calls=%async_computation.11 | async-start | bytes 3145728 | tf_op jit(solution)/shard_map/all_gather | solution.py:58
  51.2 31.7 %copy-start.2 = (f32[3,4,256,256]{3,2,1,0:T(8,128)S(1)}, f32[3,4,256,256]{3,2,1,0:T(8,128)}, u32[]{:S(2)}) copy-start(f32[3,4,256,256]{3,2,1,0:T(8,128)} %param.11) | copy-start | bytes 9437188
  102.2 2.9 copy-start
  122.0 2.3 copy-start.4
  135.0 2.6 copy-start.6
  149.9 38.3 %all-to-all-start.3 = ((bf16[8,4,80,256]{3,2,1,0:T(8,128)(2,1)}), bf16[8,4,80,256]{3,2,1,0:T(8,128)(2,1)}, u32[]{:S(2)}, u32[]{:S(2)}) async-start(bf16[8,4,80,256]{3,2,1,0:T(8,128)(2,1)} %copy.221), calls=%async_computation.3 | async-start | bytes 2621440 | tf_op jit(solution)/shard_map/all_to_all | solution.py:102
  188.2 64.2 %all-to-all-start.5 = ((bf16[8,4,80,512]{3,2,1,0:T(8,128)(2,1)}), bf16[8,4,80,512]{3,2,1,0:T(8,128)(2,1)}, u32[]{:S(2)}, u32[]{:S(2)}) async-start(bf16[8,4,80,512]{3,2,1,0:T(8,128)(2,1)} %copy.225), calls=%async_computation.5 | async-start | bytes 5242880 | tf_op jit(solution)/shard_map/all_to_all | solution.py:102
  192.6 131.4 %all-gather.6.cloned.1.call-start = ((), (), s32[]{:S(2)}) async-start(), calls=%async_computation.9 | async-start | bytes 8355840 | tf_op jit(solution)/shard_map/all_gather | solution.py:128
  254.5 69.4 %copy-start.10 = (bf16[4,256,256]{2,1,0:T(8,128)(2,1)S(1)}, bf16[4,256,256]{2,1,0:T(8,128)(2,1)}, u32[]{:S(2)}) copy-start(bf16[4,256,256]{2,1,0:T(8,128)(2,1)} %get-tuple-element.57) | copy-start | bytes 1572868
  254.5 69.4 %copy-start.11 = (bf16[4,256,256]{2,1,0:T(8,128)(2,1)S(1)}, bf16[4,256,256]{2,1,0:T(8,128)(2,1)}, u32[]{:S(2)}) copy-start(bf16[4,256,256]{2,1,0:T(8,128)(2,1)} %get-tuple-element.58) | copy-start | bytes 1572868
  258.5 73.2 %all-to-all-start.8 = ((bf16[2,2,128]{2,1,0:T(2,128)(2,1)}), bf16[2,2,128]{2,1,0:T(2,128)(2,1)S(1)}, u32[]{:S(2)}, u32[]{:S(2)}) async-start(bf16[2,2,128]{2,1,0:T(2,128)(2,1)} %reshape.218), calls=%async_computation.8 | async-start | bytes 2048 | tf_op jit(solution)/shard_map/all_to_all | solution.py:137
  328.0 1.3 copy-start.1
  331.6 30.4 %all-to-all-start.6 = ((bf16[16,2,128,256]{3,2,0,1:T(8,128)(2,1)}), bf16[16,2,128,256]{3,2,0,1:T(8,128)(2,1)}, u32[]{:S(2)}, u32[]{:S(2)}) async-start(bf16[16,2,128,256]{3,2,0,1:T(8,128)(2,1)} %copy.229), calls=%async_computation.6 | async-start | bytes 4194304 | tf_op jit(solution)/shard_map/all_to_all | solution.py:146
  337.2 32.6 %copy-start.7 = (bf16[32,4,40,256]{3,2,0,1:T(8,128)(2,1)S(1)}, bf16[32,4,40,256]{3,2,0,1:T(8,128)(2,1)}, u32[]{:S(2)}) copy-start(bf16[32,4,40,256]{3,2,0,1:T(8,128)(2,1)} %copy.222) | copy-start | bytes 7864324
  365.3 31.2 %all-to-all-start.7 = ((bf16[16,128,256]{2,1,0:T(8,128)(2,1)}), bf16[16,128,256]{2,1,0:T(8,128)(2,1)}, u32[]{:S(2)}, u32[]{:S(2)}) async-start(bf16[16,128,256]{2,1,0:T(8,128)(2,1)} %reduce_sum.121), calls=%async_computation.7 | async-start | bytes 2097152 | tf_op jit(solution)/shard_map/all_to_all | solution.py:148
  369.9 8.9 %copy-start.9 = (f32[3,4,256,256]{3,2,1,0:T(8,128)S(1)}, f32[3,4,256,256]{3,2,1,0:T(8,128)}, u32[]{:S(2)}) copy-start(f32[3,4,256,256]{3,2,1,0:T(8,128)} %param.13) | copy-start | bytes 9437188
  374.1 1.7 copy-start.5
  375.8 2.9 copy-start.3
  375.8 3.6 copy-start.8
Sparse Core Ops, SparseCore 0:
  51.3 33.0 all-gather.7
  85.9 33.0 all-gather.9
  256.5 67.3 all-gather.5
